TPU v7x, 32 devices: a whole 2x2x4 slice. The times are simulated.
32 devices in a mesh: dp: 8 (over y, x, core), tp: 4 (over z).
Axes of the slice: x: 2, y: 2, z: 4, core: 2. Of those that a mesh axis runs over, the one named last changes fastest.
Arguments:
- patches: bfloat16 [16384, 768], P(('dp', 'tp')), may hold values from -6 to 6
- validity: int32 [16, 1024], P('dp'), may hold values from 0 to 1, as said below
- mask_pos: int32 [16, 1024], P('dp'), may hold values 0 or 1
- mask_token: float32 [768], replicated, may hold values from -5 to 5
- ln1_gain: float32 [768], replicated, may hold values from 0.5 to 1.5
- ln1_bias: float32 [768], replicated, may hold values from -3 to 3
- w_qkv: bfloat16 [768, 3, 768], P(None, None, 'tp'), may hold values from -0.21875 to 0.21875
- b_qv: float32 [2, 768], P(None, 'tp'), may hold values from -3 to 3
- w_out: bfloat16 [768, 768], P('tp'), may hold values from -0.625 to 0.625
- b_out: float32 [768], replicated, may hold values from -3 to 3
- ln2_gain: float32 [768], replicated, may hold values from 0.5 to 1.5
- ln2_bias: float32 [768], replicated, may hold values from -3 to 3
- w_up: bfloat16 [768, 3072], P(None, 'tp'), may hold values from -0.21875 to 0.21875
- b_up: float32 [3072], P('tp'), may hold values from -3 to 3
- w_down: bfloat16 [3072, 768], P('tp'), may hold values from -0.109375 to 0.109375
- b_down: float32 [768], replicated, may hold values from -3 to 3
- out_grad: bfloat16 [16384, 768], P(('dp', 'tp')), may hold values from -6 to 6
Outputs:
- output: bfloat16 [16384, 768], P(('dp', 'tp'))
- grad_patches: float32 [16384, 768], P(('dp', 'tp'))
- grad_mask_token: float32 [768], replicated
- grad_ln1_gain: float32 [768], replicated
- grad_ln1_bias: float32 [768], replicated
- grad_w_qkv: float32 [768, 3, 768], P(None, None, 'tp')
- grad_b_qv: float32 [2, 768], P(None, 'tp')
- grad_w_out: float32 [768, 768], P('tp')
- grad_b_out: float32 [768], replicated
- grad_ln2_gain: float32 [768], replicated
- grad_ln2_bias: float32 [768], replicated
- grad_w_up: float32 [768, 3072], P(None, 'tp')
- grad_b_up: float32 [3072], P('tp')
- grad_w_down: float32 [3072, 768], P('tp')
- grad_b_down: float32 [768], replicated
Inputs may be any that keep to these rules, and one draw needn't show every extreme that they name: `validity`: each bucket's valid slots are its first ones, at least 256 of them; buckets whose index is a multiple of 3 are full.
All inputs are finite; a program needn't handle non-finite values. No bound on the sum of `mask_pos` on one device may be relied on, other than what follows from the above.
Results may differ from a plain program's by a relative error of at most 0.017.
Values may be sent and summed in bfloat16 or wider, within the bound.
A program may use at most 128 MiB of HBM per device.

v0:
```python
import jax
import jax.numpy as jnp
from jax import lax
from jax.sharding import PartitionSpec as P

HEAD_DIM = 64


def layer_norm(values, gain, bias):
    center = values - jnp.mean(values, -1, keepdims=True)
    spread = jnp.mean(center * center, -1, keepdims=True)
    return center * lax.rsqrt(spread + 1e-06) * gain + bias


def exact_gelu(values):
    return jax.nn.gelu(values, approximate=False)


def outer_sum(left, right):
    return lax.dot_general(
        left, right, (((0,), (0,)), ((), ())), preferred_element_type=jnp.float32
    )


def dot_trans(left, right):
    return lax.dot_general(
        left, right, (((1,), (1,)), ((), ())), preferred_element_type=jnp.float32
    )


def masked_scores(query_rows, key_rows, keep_key):
    scores = jnp.einsum(
        "qhd,khd->hqk", query_rows, key_rows, preferred_element_type=jnp.float32
    ) * HEAD_DIM ** (-0.5)
    return jnp.where(keep_key[None, None, :] > 0, scores, -1000000000.0)


def attend(bucket_in):
    packed, keep_key = bucket_in
    scores = masked_scores(packed[:, 0], packed[:, 1], keep_key)
    row_max = jnp.max(scores, -1, keepdims=True)
    powered = jnp.exp(scores - row_max)
    row_sum = jnp.sum(powered, -1, keepdims=True)
    weights = (powered / row_sum).astype(jnp.bfloat16)
    context = jnp.einsum("hqk,khd->qhd", weights, packed[:, 2], preferred_element_type=jnp.float32)
    return (context.astype(jnp.bfloat16), (row_max + jnp.log(row_sum))[..., 0])


def attend_back(bucket_in):
    packed, keep_key, log_norm, grad_ctx = bucket_in
    query_rows, key_rows, value_rows = (packed[:, 0], packed[:, 1], packed[:, 2])
    scale_factor = HEAD_DIM ** (-0.5)
    weights = jnp.exp(masked_scores(query_rows, key_rows, keep_key) - log_norm[..., None])
    grad_weights = jnp.einsum(
        "qhd,khd->hqk", grad_ctx, value_rows, preferred_element_type=jnp.float32
    )
    inner = jnp.sum(weights * grad_weights, -1, keepdims=True)
    grad_scores = (weights * (grad_weights - inner)).astype(jnp.bfloat16)
    grad_query = (
        jnp.einsum("hqk,khd->qhd", grad_scores, key_rows, preferred_element_type=jnp.float32)
        * scale_factor
    )
    grad_key = (
        jnp.einsum("hqk,qhd->khd", grad_scores, query_rows, preferred_element_type=jnp.float32)
        * scale_factor
    )
    grad_value = jnp.einsum(
        "hqk,qhd->khd", weights.astype(jnp.bfloat16), grad_ctx, preferred_element_type=jnp.float32
    )
    return jnp.stack([grad_query, grad_key, grad_value], 1).astype(jnp.bfloat16)


def shards(
    patches,
    validity,
    mask_pos,
    mask_token,
    ln1_gain,
    ln1_bias,
    w_qkv,
    b_qv,
    w_out,
    b_out,
    ln2_gain,
    ln2_bias,
    w_up,
    b_up,
    w_down,
    b_down,
    out_grad,
):
    row_count = patches.shape[0]
    model_width = patches.shape[1]
    buckets = validity.shape[0]
    seq_len = validity.shape[1]
    local_width = w_qkv.shape[2]
    local_heads = local_width // HEAD_DIM
    group_rows = buckets * seq_len
    row_start = lax.axis_index("tp") * row_count
    valid_col = lax.dynamic_slice_in_dim(validity.reshape(-1), row_start, row_count).astype(
        jnp.float32
    )[:, None]
    masked_col = lax.dynamic_slice_in_dim(mask_pos.reshape(-1), row_start, row_count).astype(
        jnp.float32
    )[:, None]
    keep_token = valid_col * (1.0 - masked_col)
    swap_token = valid_col * masked_col
    block_in = keep_token * patches.astype(jnp.float32) + swap_token * mask_token[None, :]
    normed_f, ln1_pull = jax.vjp(layer_norm, block_in, ln1_gain, ln1_bias)
    normed_one = normed_f.astype(jnp.bfloat16)
    normed_all = lax.all_gather(normed_one, "tp", axis=0, tiled=True)
    flat_qkv = w_qkv.reshape(model_width, 3 * local_width)
    qkv_rows = jnp.dot(normed_all, flat_qkv, preferred_element_type=jnp.float32).reshape(
        group_rows, 3, local_width
    )
    qkv_bias = jnp.stack([b_qv[0], jnp.zeros_like(b_qv[0]), b_qv[1]])
    qkv_rows = (qkv_rows + qkv_bias[None]).astype(jnp.bfloat16)
    heads_view = qkv_rows.reshape(buckets, seq_len, 3, local_heads, HEAD_DIM)
    context, log_norm = lax.map(attend, (heads_view, validity))
    context = context.reshape(group_rows, local_width)
    attn_part = jnp.dot(context, w_out, preferred_element_type=jnp.float32).astype(jnp.bfloat16)
    attn_rows = lax.psum_scatter(attn_part, "tp", scatter_dimension=0, tiled=True).astype(
        jnp.float32
    )
    residual = block_in + attn_rows + b_out[None, :]
    normed_g, ln2_pull = jax.vjp(layer_norm, residual, ln2_gain, ln2_bias)
    normed_two = normed_g.astype(jnp.bfloat16)
    normed_mlp = lax.all_gather(normed_two, "tp", axis=0, tiled=True)
    hidden_pre = jnp.dot(normed_mlp, w_up, preferred_element_type=jnp.float32) + b_up[None, :]
    gelu_out, gelu_pull = jax.vjp(exact_gelu, hidden_pre)
    hidden = gelu_out.astype(jnp.bfloat16)
    mlp_part = jnp.dot(hidden, w_down, preferred_element_type=jnp.float32).astype(jnp.bfloat16)
    mlp_rows = lax.psum_scatter(mlp_part, "tp", scatter_dimension=0, tiled=True).astype(jnp.float32)
    output = (valid_col * (residual + mlp_rows + b_down[None, :])).astype(jnp.bfloat16)
    grad_out = valid_col * out_grad.astype(jnp.float32)
    grad_b_down = jnp.sum(grad_out, 0)
    grad_out_all = lax.all_gather(grad_out.astype(jnp.bfloat16), "tp", axis=0, tiled=True)
    grad_w_down = outer_sum(hidden, grad_out_all)
    grad_hid = dot_trans(grad_out_all, w_down)
    grad_pre = gelu_pull(grad_hid)[0].astype(jnp.bfloat16)
    grad_w_up = outer_sum(normed_mlp, grad_pre)
    grad_b_up = jnp.sum(grad_pre.astype(jnp.float32), 0)
    grad_normed_two = lax.psum_scatter(
        dot_trans(grad_pre, w_up).astype(jnp.bfloat16), "tp", scatter_dimension=0, tiled=True
    ).astype(jnp.float32)
    grad_res_part, grad_ln2_gain, grad_ln2_bias = ln2_pull(grad_normed_two)
    grad_res = grad_out + grad_res_part
    grad_b_out = jnp.sum(grad_res, 0)
    grad_res_all = lax.all_gather(grad_res.astype(jnp.bfloat16), "tp", axis=0, tiled=True)
    grad_w_out = outer_sum(context, grad_res_all)
    grad_context = dot_trans(grad_res_all, w_out).astype(jnp.bfloat16)
    grad_heads = lax.map(
        attend_back,
        (
            heads_view,
            validity,
            log_norm,
            grad_context.reshape(buckets, seq_len, local_heads, HEAD_DIM),
        ),
    )
    grad_qkv = grad_heads.reshape(group_rows, 3 * local_width)
    grad_w_qkv = outer_sum(normed_all, grad_qkv).reshape(model_width, 3, local_width)
    column_sums = jnp.sum(grad_qkv.astype(jnp.float32), 0).reshape(3, local_width)
    grad_b_qv = jnp.stack([column_sums[0], column_sums[2]])
    grad_normed_one = lax.psum_scatter(
        dot_trans(grad_qkv, flat_qkv).astype(jnp.bfloat16), "tp", scatter_dimension=0, tiled=True
    ).astype(jnp.float32)
    grad_in_part, grad_ln1_gain, grad_ln1_bias = ln1_pull(grad_normed_one)
    grad_in = grad_res + grad_in_part
    grad_patches = keep_token * grad_in
    grad_mask_token = jnp.sum(swap_token * grad_in, 0)
    grad_w_qkv, grad_b_qv, grad_w_out, grad_w_up, grad_b_up, grad_w_down = lax.psum(
        (grad_w_qkv, grad_b_qv, grad_w_out, grad_w_up, grad_b_up, grad_w_down), "dp"
    )
    (
        grad_mask_token,
        grad_ln1_gain,
        grad_ln1_bias,
        grad_b_out,
        grad_ln2_gain,
        grad_ln2_bias,
        grad_b_down,
    ) = lax.psum(
        (
            grad_mask_token,
            grad_ln1_gain,
            grad_ln1_bias,
            grad_b_out,
            grad_ln2_gain,
            grad_ln2_bias,
            grad_b_down,
        ),
        ("dp", "tp"),
    )
    return (
        output,
        grad_patches,
        grad_mask_token,
        grad_ln1_gain,
        grad_ln1_bias,
        grad_w_qkv,
        grad_b_qv,
        grad_w_out,
        grad_b_out,
        grad_ln2_gain,
        grad_ln2_bias,
        grad_w_up,
        grad_b_up,
        grad_w_down,
        grad_b_down,
    )


def solution(mesh):
    return jax.shard_map(
        shards,
        mesh=mesh,
        in_specs=(
            P(("dp", "tp"), None),
            P("dp", None),
            P("dp", None),
            P(),
            P(),
            P(),
            P(None, None, "tp"),
            P(None, "tp"),
            P("tp", None),
            P(),
            P(),
            P(),
            P(None, "tp"),
            P("tp"),
            P("tp", None),
            P(),
            P(("dp", "tp"), None),
        ),
        out_specs=(
            P(("dp", "tp"), None),
            P(("dp", "tp"), None),
            P(),
            P(),
            P(),
            P(None, None, "tp"),
            P(None, "tp"),
            P("tp", None),
            P(),
            P(),
            P(),
            P(None, "tp"),
            P("tp"),
            P("tp", None),
            P(),
        ),
        check_vma=False,
    )
```

profile of v0, /device:TPU:0, one launch (start us, length us, event | category | flops | bytes accessed | tf_op | source)
XLA Modules:
  0.0 791.8 jit_solution(12632221873132776220)
XLA Ops:
  10.4 1.7 multiply_reduce_fusion.3
  13.2 3.4 add_convert_fusion.3
  17.0 65.9 %all-gather.5.cloned.1.call-done = bf16[2048,768]{1,0:T(8,128)(2,1)} async-done(((bf16[512,768]{1,0:T(8,128)(2,1)}), bf16[2048,768]{1,0:T(8,128)(2,1)}) %all-gather.5.cloned.1.call-update) | async-done | bytes 3145744 | tf_op jit(solution)/shard_map/all_gather | solution.py:111
  83.0 4.1 add_convert_fusion.1
  87.1 2.9 reshape.235
  90.1 2.4 copy.43
  92.5 22.2 %while.22 = (s32[]{:T(128)}, bf16[2,1024,3,64]{1,3,2,0:T(8,128)(2,1)}, f32[2,3,1024]{2,1,0:T(4,128)}, bf16[2,1024,3,3,64]{1,4,3,2,0:T(8,128)(2,1)S(1)}, s32[2,1024]{1,0:T(2,128)}, /*index=5*/s32[]{:T(128)}) while((s32[]{:T(128)}, bf16[2,1024,3,64]{1,3,2,0:T(8,128)(2,1)}, f32[2,3,1024]{2,1,0:T(4,128)}, ...), condition=%wide.region_5.6_spmd, body=%wide.region_2.5_spmd.sunk | while | flops 843249664 | bytes 48296140 | solution.py:119
  93.3 2.4 fusion.107
  95.7 3.2 fusion.108
  98.9 3.2 fusion.109
  104.4 2.4 fusion.107
  106.8 3.2 fusion.108
  110.0 3.2 fusion.109
  114.7 2.6 copy.44
  118.4 2.7 convolution_convert_fusion.3
  121.3 58.9 %reduce-scatter.5.cloned.1.call-done = bf16[512,768]{1,0:T(8,128)(2,1)} async-done(((bf16[2048,768]{1,0:T(8,128)(2,1)}), bf16[512,768]{1,0:T(8,128)(2,1)}) %reduce-scatter.5.cloned.1.call-update) | async-done | bytes 786448 | tf_op jit(solution)/shard_map/reduce_scatter | solution.py:122
  180.3 1.9 fusion.62
  182.2 2.0 multiply_reduce_fusion.2
  185.4 3.1 add_convert_fusion.2
  188.5 1.8 fusion.54
  190.3 61.6 %all-gather.7.cloned.1.call-done = bf16[2048,768]{1,0:T(8,128)(2,1)} async-done(((bf16[512,768]{1,0:T(8,128)(2,1)}), bf16[2048,768]{1,0:T(8,128)(2,1)}) %all-gather.7.cloned.1.call-update) | async-done | bytes 3145744 | tf_op jit(solution)/shard_map/all_gather | solution.py:128
  251.9 7.5 fusion.69
  259.4 56.6 %all-gather.9.cloned.1.call-done = bf16[2048,768]{1,0:T(8,128)(2,1)} async-done(((bf16[512,768]{1,0:T(8,128)(2,1)}), bf16[2048,768]{1,0:T(8,128)(2,1)}) %all-gather.9.cloned.1.call-update) | async-done | bytes 3145744 | tf_op jit(solution)/shard_map/all_gather | solution.py:137
  316.1 20.2 %convert_reduce_fusion = (f32[768]{0:T(1024)}, bf16[2048,768]{1,0:T(8,128)(2,1)S(1)}, f32[2048,768]{1,0:T(8,128)}) fusion(f32[2048,768]{1,0:T(8,128)} %fusion.69, f32[768]{0:T(1024)} %param.34, bf16[2048,768]{1,0:T(8,128)(2,1)} %all-gather.9.cloned.1.call-done, bf16[768,768]{1,0:T(8,128)(2,1)S(1)} %copy-done), kind=kOutput, calls=%fused_computation.51 | convolution fusion | flops 2533883136 | bytes 20060160 | tf_op jit(solution)/shard_map/dot_general | solution.py:26
  336.3 1.7 copy-done.64
  338.0 4.0 convolution_convert_fusion
  342.5 5.7 multiply_convert_fusion.1
  348.2 1.7 copy-done.18
  349.9 4.0 convolution_convert_fusion.1
  354.0 47.2 %reduce-scatter.9.cloned.1.call-done = bf16[512,768]{1,0:T(8,128)(2,1)} async-done(((bf16[2048,768]{1,0:T(8,128)(2,1)}), bf16[512,768]{1,0:T(8,128)(2,1)}) %reduce-scatter.9.cloned.1.call-update) | async-done | bytes 786448 | tf_op jit(solution)/shard_map/reduce_scatter | solution.py:143
  401.2 2.8 convert_reduce_fusion.3
  404.1 1.8 fusion.51
  405.9 57.8 %reduce-scatter.7.cloned.1.call-done = bf16[512,768]{1,0:T(8,128)(2,1)} async-done(((bf16[2048,768]{1,0:T(8,128)(2,1)}), bf16[512,768]{1,0:T(8,128)(2,1)}) %reduce-scatter.7.cloned.1.call-update) | async-done | bytes 786448 | tf_op jit(solution)/shard_map/reduce_scatter | solution.py:133
  463.7 4.2 fusion.66
  468.0 63.4 %all-gather.11.cloned.1.call-done = bf16[2048,768]{1,0:T(8,128)(2,1)} async-done(((bf16[512,768]{1,0:T(8,128)(2,1)}), bf16[2048,768]{1,0:T(8,128)(2,1)}) %all-gather.11.cloned.1.call-update) | async-done | bytes 3145744 | tf_op jit(solution)/shard_map/all_gather | solution.py:149
  531.4 3.9 convolution_convert_fusion.4
  535.4 2.7 reshape.237
  539.2 51.5 %while.23 = (s32[]{:T(128)}, bf16[2,1024,3,3,64]{1,4,3,2,0:T(8,128)(2,1)}, bf16[2,1024,3,3,64]{1,4,3,2,0:T(8,128)(2,1)S(1)}, s32[2,1024]{1,0:T(2,128)S(1)}, f32[...) while((s32[]{:T(128)}, bf16[2,1024,3,3,64]{1,4,3,2,0:T(8,128)(2,1)}, ...), condition=%wide.region_15.16_spmd, body=%wide.region_13.15_spmd.sunk | while | flops 2064971776 | bytes 151884048 | solution.py:152
  540.2 1.8 fusion.114
  542.1 4.3 fusion.115
  546.4 4.8 multiply_reduce_fusion.5
  551.2 5.6 multiply_convert_fusion.4
  556.8 4.1 fusion.117
  561.4 2.0 fusion.116
  565.9 1.8 fusion.114
  567.7 4.3 fusion.115
  572.1 4.8 multiply_reduce_fusion.5
  576.8 5.6 multiply_convert_fusion.4
  582.5 4.1 fusion.117
  587.1 2.0 fusion.116
  590.7 4.1 copy.47
  595.9 4.0 convolution_convert_fusion.2
  600.3 7.1 fusion.71
  607.3 4.2 fusion.72
  611.5 1.7 fusion.70
  613.7 3.2 fusion.39
  617.0 1.6 copy-done.14
  619.3 14.2 %all-reduce.1 = (f32[2,192]{1,0:T(2,128)}, f32[768]{0:T(1024)}) all-reduce(f32[2,192]{1,0:T(2,128)S(1)} %pad_maximum_fusion.1, f32[768]{0:T(1024)S(1)} %copy-done.58), channel_id=1, replica_groups=mesh['dp'=8,'tp'=4] {'dp'}, use_global_device_ids=true, to_apply=%region_27.28 | all-reduce | flops 1152 | bytes 9216 | tf_op jit(solution)/shard_map/psum | solution.py:172
  633.5 25.6 %reduce-scatter.11.cloned.1.call-done = bf16[512,768]{1,0:T(8,128)(2,1)} async-done(((bf16[2048,768]{1,0:T(8,128)(2,1)}), bf16[512,768]{1,0:T(8,128)(2,1)}) %reduce-scatter.11.cloned.1.call-update) | async-done | bytes 786448 | tf_op jit(solution)/shard_map/reduce_scatter | solution.py:165
  659.2 2.1 fusion.52
  661.3 2.1 fusion.65
  665.1 41.6 %all-reduce = (f32[768]{0:T(1024)}, f32[768]{0:T(1024)}, f32[768]{0:T(1024)}, f32[768]{0:T(1024)}, f32[768]{0:T(1024)}, /*index=5*/f32[768]{0:T(1024)}, f32[768]{0:T(1024)}) all-reduce(f32[768]{0:T(1024)S(1)} %get-tuple-element.105, f32[768]{0:T(1024)S(1)} %get-tuple-element.102, ...), channel_id=1, replica_groups=mesh['dp'=8,'tp'=4] {'dp','tp'}, use_global_device_ids=true, to_apply=%region_20.21 | all-reduce | flops 5376 | bytes 43008 | tf_op jit(solution)/shard_map/psum | solution.py:183
  706.7 70.6 %all-reduce.5.cloned.1.call-done = (f32[768,3,192]{0,2,1:T(8,128)}, f32[192,768]{1,0:T(8,128)}, f32[768,768]{1,0:T(8,128)}, f32[768,768]{1,0:T(8,128)}) async-done(((f32[768,3,192]{0,2,1:T(8,128)}, f32[192,768]{1,0:T(8,128)}, f32[768,768]{1,0:T(8,128)}, f32[768,768]{1,0:T(8,128)}), (f32[768,3,192]{0,2,1:T(8,128)}, f32[192,768]{1,0:T(8,128)}, f32[768,768]{1,0:T(8,128)}, ...) | async-done | bytes 7077904 | tf_op jit(solution)/shard_map/psum | solution.py:172
  777.3 2.9 copy.82
  (207 shorter events, 28.4 us)
Async XLA Ops:
  7.2 308.9 %copy-start = (bf16[768,768]{1,0:T(8,128)(2,1)S(1)}, bf16[768,768]{1,0:T(8,128)(2,1)}, u32[]{:S(2)}) copy-start(bf16[768,768]{1,0:T(8,128)(2,1)} %param.35) | copy-start | bytes 3538948
  7.2 9.8 %copy-start.59 = (f32[2,192]{1,0:T(2,128)S(1)}, f32[2,192]{1,0:T(2,128)}, u32[]{:S(2)}) copy-start(f32[2,192]{1,0:T(2,128)} %param.28) | copy-start | bytes 4612
  7.2 75.8 %all-gather.5.cloned.1.call-start = ((), (), s32[]{:S(2)}) async-start(), calls=%async_computation.4 | async-start | bytes 3932160 | tf_op jit(solution)/shard_map/all_gather | solution.py:111
  8.1 455.6 %copy-start.28 = (f32[512]{0:T(512)}, f32[512]{0:T(512)S(1)}, u32[]{:S(2)}) copy-start(f32[512]{0:T(512)S(1)} %get-tuple-element.151) | copy-start | bytes 6148
  8.8 454.9 %copy-start.30 = (f32[512]{0:T(512)}, f32[512]{0:T(512)S(1)}, u32[]{:S(2)}) copy-start(f32[512]{0:T(512)S(1)} %convert_multiply_fusion.5) | copy-start | bytes 6148
  10.4 2.3 copy-start.41
  16.6 163.6 %reduce-scatter.5.cloned.1.call-start = ((), (), s32[]{:S(2)}) async-start(), calls=%async_computation.5 | async-start | bytes 3932160 | tf_op jit(solution)/shard_map/reduce_scatter | solution.py:122
  95.7 3.2 copy-start.23
  98.9 3.2 copy-start.35
  106.8 3.2 copy-start.23
  110.0 3.2 copy-start.35
  114.7 2.8 copy-start.5
  114.7 3.7 copy-start.33
  121.0 59.2 %copy-start.3 = (bf16[512,768]{1,0:T(8,128)(2,1)S(1)}, bf16[512,768]{1,0:T(8,128)(2,1)}, u32[]{:S(2)}) copy-start(bf16[512,768]{1,0:T(8,128)(2,1)} %param.21) | copy-start | bytes 2359300
  121.0 59.2 %copy-start.26 = (f32[768]{0:T(1024)S(1)}, f32[768]{0:T(1024)}, u32[]{:S(2)}) copy-start(f32[768]{0:T(1024)} %param.24) | copy-start | bytes 9220
  121.0 59.2 %copy-start.37 = (f32[768]{0:T(1024)S(1)}, f32[768]{0:T(1024)}, u32[]{:S(2)}) copy-start(f32[768]{0:T(1024)} %param.30) | copy-start | bytes 9220
  121.1 130.9 %all-gather.7.cloned.1.call-start = ((), (), s32[]{:S(2)}) async-start(), calls=%async_computation.6 | async-start | bytes 3932160 | tf_op jit(solution)/shard_map/all_gather | solution.py:128
  180.3 5.1 copy-start.7
  182.2 2.6 copy-start.38
  182.2 6.3 copy-start.20
  188.4 127.6 %all-gather.9.cloned.1.call-start = ((), (), s32[]{:S(2)}) async-start(), calls=%async_computation.8 | async-start | bytes 3932160 | tf_op jit(solution)/shard_map/all_gather | solution.py:137
  190.3 210.9 %reduce-scatter.9.cloned.1.call-start = ((), (), s32[]{:S(2)}) async-start(), calls=%async_computation.9 | async-start | bytes 3932160 | tf_op jit(solution)/shard_map/reduce_scatter | solution.py:143
  316.1 21.9 %copy-start.62 = (bf16[768,768]{1,0:T(8,128)(2,1)S(1)}, bf16[768,768]{1,0:T(8,128)(2,1)}, u32[]{:S(2)}) copy-start(bf16[768,768]{1,0:T(8,128)(2,1)} %param.33) | copy-start | bytes 3538948
  342.0 121.7 %reduce-scatter.7.cloned.1.call-start = ((), (), s32[]{:S(2)}) async-start(), calls=%async_computation.7 | async-start | bytes 3932160 | tf_op jit(solution)/shard_map/reduce_scatter | solution.py:133
  348.2 1.7 copy-start.18
  353.9 47.3 %copy-start.39 = (f32[512]{0:T(512)S(1)}, f32[512]{0:T(512)}, u32[]{:S(2)}) copy-start(f32[512]{0:T(512)} %copy-done.38) | copy-start | bytes 6148
  353.9 47.3 %copy-start.40 = (f32[768]{0:T(1024)S(1)}, f32[768]{0:T(1024)}, u32[]{:S(2)}) copy-start(f32[768]{0:T(1024)} %param.31) | copy-start | bytes 9220
  353.9 50.1 %copy-start.53 = (f32[512]{0:T(512)S(1)}, f32[512]{0:T(512)}, u32[]{:S(2)}) copy-start(f32[512]{0:T(512)} %copy-done.52) | copy-start | bytes 6148
  353.9 50.1 %copy-start.47 = (f32[512]{0:T(512)S(1)}, f32[512]{0:T(512)}, u32[]{:S(2)}) copy-start(f32[512]{0:T(512)} %copy-done.46) | copy-start | bytes 6148
  353.9 109.8 %copy-start.49 = (f32[512]{0:T(512)S(1)}, f32[512]{0:T(512)}, u32[]{:S(2)}) copy-start(f32[512]{0:T(512)} %copy-done.48) | copy-start | bytes 6148
  354.0 109.8 %copy-start.57 = (f32[768]{0:T(1024)S(1)}, f32[768]{0:T(1024)}, u32[]{:S(2)}) copy-start(f32[768]{0:T(1024)} %param.36) | copy-start | bytes 9220
  354.0 177.5 %all-gather.11.cloned.1.call-start = ((), (), s32[]{:S(2)}) async-start(), calls=%async_computation.10 | async-start | bytes 3932160 | tf_op jit(solution)/shard_map/all_gather | solution.py:149
  401.2 2.9 copy-start.15
  405.9 125.5 %copy-start.34 = (bf16[192,768]{1,0:T(8,128)(2,1)S(1)}, bf16[192,768]{1,0:T(8,128)(2,1)}, u32[]{:S(2)}) copy-start(bf16[192,768]{1,0:T(8,128)(2,1)} %param.29) | copy-start | bytes 884740
  467.9 191.3 %reduce-scatter.11.cloned.1.call-start = ((), (), s32[]{:S(2)}) async-start(), calls=%async_computation.11 | async-start | bytes 3932160 | tf_op jit(solution)/shard_map/reduce_scatter | solution.py:165
  535.4 3.8 copy-start.6
  535.4 3.8 copy-start.32
  540.2 1.9 copy-start.11
  556.8 4.6 copy-start.2
  561.4 2.0 copy-start.10
  561.4 2.1 copy-start.12
  565.9 1.9 copy-start.11
  582.4 4.6 copy-start.2
  587.0 2.1 copy-start.10
  587.1 2.1 copy-start.12
  600.0 177.3 %all-reduce.5.cloned.1.call-start = ((), (), s32[]{:S(2)}) async-start(), calls=%async_computation.12 | async-start | bytes 14155776 | tf_op jit(solution)/shard_map/psum | solution.py:172
  600.2 7.1 copy-start.19
  600.3 7.1 copy-start.61
  607.3 4.2 copy-start.9
  607.3 4.2 copy-start.17
  611.5 2.2 copy-start.60
  618.6 40.6 %copy-start.4 = (bf16[512,768]{1,0:T(8,128)(2,1)S(1)}, bf16[512,768]{1,0:T(8,128)(2,1)}, u32[]{:S(2)}) copy-start(bf16[512,768]{1,0:T(8,128)(2,1)} %param.21) | copy-start | bytes 2359300
  618.6 40.6 %copy-start.27 = (f32[768]{0:T(1024)S(1)}, f32[768]{0:T(1024)}, u32[]{:S(2)}) copy-start(f32[768]{0:T(1024)} %param.24) | copy-start | bytes 9220
  618.6 40.6 %copy-start.29 = (f32[512]{0:T(512)S(1)}, f32[512]{0:T(512)}, u32[]{:S(2)}) copy-start(f32[512]{0:T(512)} %copy-done.28) | copy-start | bytes 6148
  618.6 40.6 %copy-start.31 = (f32[512]{0:T(512)S(1)}, f32[512]{0:T(512)}, u32[]{:S(2)}) copy-start(f32[512]{0:T(512)} %copy-done.30) | copy-start | bytes 6148
  618.6 40.6 %copy-start.42 = (f32[512]{0:T(512)S(1)}, f32[512]{0:T(512)}, u32[]{:S(2)}) copy-start(f32[512]{0:T(512)} %copy-done.41) | copy-start | bytes 6148
  618.6 40.6 %copy-start.43 = (f32[768]{0:T(1024)S(1)}, f32[768]{0:T(1024)}, u32[]{:S(2)}) copy-start(f32[768]{0:T(1024)} %param.25) | copy-start | bytes 9220
  618.7 40.6 %copy-start.45 = (f32[512]{0:T(512)S(1)}, f32[512]{0:T(512)}, u32[]{:S(2)}) copy-start(f32[512]{0:T(512)} %copy-done.44) | copy-start | bytes 6148
  618.7 42.6 %copy-start.51 = (f32[512]{0:T(512)S(1)}, f32[512]{0:T(512)}, u32[]{:S(2)}) copy-start(f32[512]{0:T(512)} %copy-done.50) | copy-start | bytes 6148
  633.5 29.9 %copy-start.16 = (f32[512,768]{1,0:T(8,128)S(1)}, f32[512,768]{1,0:T(8,128)}, u32[]{:S(2)}) copy-start(f32[512,768]{1,0:T(8,128)} %get-tuple-element.150) | copy-start | bytes 4718596
  777.3 3.0 copy-start.25
  777.3 3.8 copy-start.22
  781.1 2.5 copy-start.21
  781.1 3.9 copy-start.1
  (19 other events, 19.6 us)
Sparse Core Ops, SparseCore 0:
  16.8 66.1 all-gather.4
  121.2 59.0 reduce-scatter.4
  188.6 63.3 all-gather.6
  253.9 62.0 all-gather.8
  342.1 59.0 reduce-scatter.8
  403.4 60.2 reduce-scatter.6
  468.0 63.3 all-gather.10
  600.1 59.0 reduce-scatter.10
  664.0 113.2 all-reduce.4
where the time goes:
time: 795 us; the launch traced here: 792 us
  waiting for transfers between devices  508 us (64%)
  matrix products  112 us (14%)
  blocking collectives  55.9 us (7%)
  other arithmetic  55.7 us (7%)
  local copies, waits for them, and re-layouts  43.9 us (6%)
  between operations  14.5 us (2%)
    psum x1, waiting for transfers between devices, shards(): lax.psum((grad_w_qkv, grad_b_qv, grad_w_out, grad_w_up, grad_b_up, grad_w...  70.6 us
    all_gather x1, waiting for transfers between devices, shards(): normed_all = lax.all_gather(normed_one, 'tp', axis=0, tiled=True)  65.9 us
    all_gather x1, waiting for transfers between devices, shards(): lax.all_gather(grad_res.astype(jnp.bfloat16), 'tp', axis=0, tiled=True)  63.4 us
    all_gather x1, waiting for transfers between devices, shards(): normed_mlp = lax.all_gather(normed_two, 'tp', axis=0, tiled=True)  61.6 us
    reduce_scatter x1, waiting for transfers between devices, shards(): lax.psum_scatter(attn_part, 'tp', scatter_dimension=0, tiled=True)  58.9 us
    reduce_scatter x1, waiting for transfers between devices, shards(): lax.psum_scatter(mlp_part, 'tp', scatter_dimension=0, tiled=True)  57.8 us
    all_gather x1, waiting for transfers between devices, shards(): lax.all_gather(grad_out.astype(jnp.bfloat16), 'tp', axis=0, tiled=True)  56.6 us
    reduce_scatter x1, waiting for transfers between devices, shards(): lax.psum_scatter(dot_trans(grad_pre, w_up).astype(jnp.bfloat16), 'tp', sc...  47.2 us
  transfers between devices with their start and end apart: 9, of which 9 were waited for; matrix products, arithmetic and copies ran while one was open for 6% of the time, Pallas kernels for 0%

commit v1 on v0

--- a/solution.py
+++ b/solution.py
@@ -4,6 +4,18 @@
 from jax.sharding import PartitionSpec as P
 
 HEAD_DIM = 64
+
+
+def doubled_up(shard, axis, dim):
+    ways, here = (lax.axis_size(axis), lax.axis_index(axis))
+    grown, reach = (shard, 1)
+    while reach < ways:
+        theirs = lax.ppermute(grown, axis, [(d, d ^ reach) for d in range(ways)])
+        mine_first = jnp.concatenate([grown, theirs], axis=dim)
+        theirs_first = jnp.concatenate([theirs, grown], axis=dim)
+        grown = jnp.where(here & reach == 0, mine_first, theirs_first)
+        reach = 2 * reach
+    return grown
 
 
 def layer_norm(values, gain, bias):
@@ -108,7 +120,7 @@
     block_in = keep_token * patches.astype(jnp.float32) + swap_token * mask_token[None, :]
     normed_f, ln1_pull = jax.vjp(layer_norm, block_in, ln1_gain, ln1_bias)
     normed_one = normed_f.astype(jnp.bfloat16)
-    normed_all = lax.all_gather(normed_one, "tp", axis=0, tiled=True)
+    normed_all = doubled_up(normed_one, "tp", 0)
     flat_qkv = w_qkv.reshape(model_width, 3 * local_width)
     qkv_rows = jnp.dot(normed_all, flat_qkv, preferred_element_type=jnp.float32).reshape(
         group_rows, 3, local_width

time: 795 us -> 826 us (1.039)
  waiting for transfers between devices: 508 us -> 528 us
    ppermute x0 -> x2, waiting for transfers between devices: none -> 85 us  [doubled_up(): theirs = lax.ppermute(grown, axis, [(d, d ^ reach) for d in range(ways)])]
    all_gather x1 -> x0, waiting for transfers between devices: 65.9 us -> none  [shards(): normed_all = lax.all_gather(normed_one, 'tp', axis=0, tiled=True)]
    unnamed x118 -> x120, local copies, waits for them, and re-layouts: 18.5 us -> 17 us
  transfers between devices with their start and end apart: 9 -> 10, of which waited for: 9 -> 10; matrix products, arithmetic and copies ran while one was open for 6% -> 6% of each run, Pallas kernels for 0% -> 0%
where the time goes in v1:
time: 826 us; the launch traced here: 821 us
  waiting for transfers between devices  528 us (64%)
  matrix products  115 us (14%)
  other arithmetic  56.8 us (7%)
  blocking collectives  56.3 us (7%)
  local copies, waits for them, and re-layouts  42.5 us (5%)
  between operations  14.8 us (2%)
    ppermute x2, waiting for transfers between devices, doubled_up(): theirs = lax.ppermute(grown, axis, [(d, d ^ reach) for d in range(ways)])  85 us
    psum x1, waiting for transfers between devices, shards(): lax.psum((grad_w_qkv, grad_b_qv, grad_w_out, grad_w_up, grad_b_up, grad_w...  70.6 us
    all_gather x1, waiting for transfers between devices, shards(): lax.all_gather(grad_res.astype(jnp.bfloat16), 'tp', axis=0, tiled=True)  63.4 us
    all_gather x1, waiting for transfers between devices, shards(): normed_mlp = lax.all_gather(normed_two, 'tp', axis=0, tiled=True)  61.6 us
    reduce_scatter x1, waiting for transfers between devices, shards(): lax.psum_scatter(attn_part, 'tp', scatter_dimension=0, tiled=True)  61.3 us
    reduce_scatter x1, waiting for transfers between devices, shards(): lax.psum_scatter(mlp_part, 'tp', scatter_dimension=0, tiled=True)  57.8 us
    all_gather x1, waiting for transfers between devices, shards(): lax.all_gather(grad_out.astype(jnp.bfloat16), 'tp', axis=0, tiled=True)  56.8 us
    reduce_scatter x1, waiting for transfers between devices, shards(): lax.psum_scatter(dot_trans(grad_pre, w_up).astype(jnp.bfloat16), 'tp', sc...  47.2 us
  transfers between devices with their start and end apart: 10, of which 10 were waited for; matrix products, arithmetic and copies ran while one was open for 6% of the time, Pallas kernels for 0%

profile of v1, /device:TPU:0, one launch (start us, length us, event | category | flops | bytes accessed | tf_op | source)
XLA Modules:
  0.0 820.8 jit_solution(14848421062115612660)
XLA Ops:
  12.1 2.5 add_convert_fusion.3
  14.7 3.1 collective-permute-start
  17.8 17.6 %collective-permute-done = bf16[512,768]{1,0:T(8,128)(2,1)} collective-permute-done((bf16[512,768]{1,0:T(8,128)(2,1)S(1)}, bf16[512,768]{1,0:T(8,128)(2,1)}, u32[]{:S(2)}, u32[]{:S(2)}) %collective-permute-start) | collective-permute-done | bytes 786464 | tf_op jit(solution)/shard_map/ppermute | solution.py:13
  35.4 1.9 maximum_select_fusion.1
  37.4 2.8 collective-permute-start.1
  40.4 67.4 %collective-permute-done.1 = bf16[1024,768]{1,0:T(8,128)(2,1)} collective-permute-done((bf16[1024,768]{1,0:T(8,128)(2,1)S(1)}, bf16[1024,768]{1,0:T(8,128)(2,1)}, u32[]{:S(2)}, u32[]{:S(2)}) %collective-permute-start.1) | collective-permute-done | bytes 1572896 | tf_op jit(solution)/shard_map/ppermute | solution.py:13
  107.7 5.3 add_convert_fusion.1
  113.1 3.1 reshape.235
  116.2 2.4 copy.43
  118.6 22.2 %while.22 = (s32[]{:T(128)}, bf16[2,1024,3,64]{1,3,2,0:T(8,128)(2,1)}, f32[2,3,1024]{2,1,0:T(4,128)}, bf16[2,1024,3,3,64]{1,4,3,2,0:T(8,128)(2,1)S(1)}, s32[2,1024]{1,0:T(2,128)}, /*index=5*/s32[]{:T(128)}) while((s32[]{:T(128)}, bf16[2,1024,3,64]{1,3,2,0:T(8,128)(2,1)}, f32[2,3,1024]{2,1,0:T(4,128)}, ...), condition=%wide.region_5.6_spmd, body=%wide.region_2.5_spmd.sunk | while | flops 843249664 | bytes 48296140 | solution.py:131
  119.4 2.4 fusion.107
  121.8 3.2 fusion.108
  125.0 3.2 fusion.109
  130.5 2.4 fusion.107
  132.9 3.2 fusion.108
  136.1 3.2 fusion.109
  140.8 2.6 copy.44
  144.5 2.7 convolution_convert_fusion.3
  147.5 61.3 %reduce-scatter.5.cloned.1.call-done = bf16[512,768]{1,0:T(8,128)(2,1)} async-done(((bf16[2048,768]{1,0:T(8,128)(2,1)}), bf16[512,768]{1,0:T(8,128)(2,1)}) %reduce-scatter.5.cloned.1.call-update) | async-done | bytes 786448 | tf_op jit(solution)/shard_map/reduce_scatter | solution.py:134
  208.8 1.9 fusion.62
  210.7 2.0 multiply_reduce_fusion.2
  213.8 3.1 add_convert_fusion.2
  217.0 1.8 fusion.52
  218.8 61.6 %all-gather.4.cloned.1.call-done = bf16[2048,768]{1,0:T(8,128)(2,1)} async-done(((bf16[512,768]{1,0:T(8,128)(2,1)}), bf16[2048,768]{1,0:T(8,128)(2,1)}) %all-gather.4.cloned.1.call-update) | async-done | bytes 3145744 | tf_op jit(solution)/shard_map/all_gather | solution.py:140
  280.4 7.5 fusion.69
  287.9 56.8 %all-gather.6.cloned.1.call-done = bf16[2048,768]{1,0:T(8,128)(2,1)} async-done(((bf16[512,768]{1,0:T(8,128)(2,1)}), bf16[2048,768]{1,0:T(8,128)(2,1)}) %all-gather.6.cloned.1.call-update) | async-done | bytes 3145744 | tf_op jit(solution)/shard_map/all_gather | solution.py:149
  344.7 20.2 %convert_reduce_fusion = (f32[768]{0:T(1024)}, bf16[2048,768]{1,0:T(8,128)(2,1)S(1)}, f32[2048,768]{1,0:T(8,128)}) fusion(f32[2048,768]{1,0:T(8,128)} %fusion.69, f32[768]{0:T(1024)} %param.34, bf16[2048,768]{1,0:T(8,128)(2,1)} %all-gather.6.cloned.1.call-done, bf16[768,768]{1,0:T(8,128)(2,1)S(1)} %copy-done), kind=kOutput, calls=%fused_computation.51 | convolution fusion | flops 2533883136 | bytes 20060160 | tf_op jit(solution)/shard_map/dot_general | solution.py:38
  364.9 1.7 copy-done.65
  366.7 4.1 convolution_convert_fusion
  371.2 5.7 multiply_convert_fusion.1
  378.7 4.0 convolution_convert_fusion.1
  382.8 47.2 %reduce-scatter.9.cloned.1.call-done = bf16[512,768]{1,0:T(8,128)(2,1)} async-done(((bf16[2048,768]{1,0:T(8,128)(2,1)}), bf16[512,768]{1,0:T(8,128)(2,1)}) %reduce-scatter.9.cloned.1.call-update) | async-done | bytes 786448 | tf_op jit(solution)/shard_map/reduce_scatter | solution.py:155
  430.0 2.8 convert_reduce_fusion.3
  432.8 1.8 fusion.49
  434.6 57.8 %reduce-scatter.7.cloned.1.call-done = bf16[512,768]{1,0:T(8,128)(2,1)} async-done(((bf16[2048,768]{1,0:T(8,128)(2,1)}), bf16[512,768]{1,0:T(8,128)(2,1)}) %reduce-scatter.7.cloned.1.call-update) | async-done | bytes 786448 | tf_op jit(solution)/shard_map/reduce_scatter | solution.py:145
  492.5 4.2 fusion.66
  496.7 63.4 %all-gather.8.cloned.1.call-done = bf16[2048,768]{1,0:T(8,128)(2,1)} async-done(((bf16[512,768]{1,0:T(8,128)(2,1)}), bf16[2048,768]{1,0:T(8,128)(2,1)}) %all-gather.8.cloned.1.call-update) | async-done | bytes 3145744 | tf_op jit(solution)/shard_map/all_gather | solution.py:161
  560.2 3.9 convolution_convert_fusion.4
  564.1 2.7 reshape.237
  567.9 51.5 %while.23 = (s32[]{:T(128)}, bf16[2,1024,3,3,64]{1,4,3,2,0:T(8,128)(2,1)}, bf16[2,1024,3,3,64]{1,4,3,2,0:T(8,128)(2,1)S(1)}, s32[2,1024]{1,0:T(2,128)S(1)}, f32[...) while((s32[]{:T(128)}, bf16[2,1024,3,3,64]{1,4,3,2,0:T(8,128)(2,1)}, ...), condition=%wide.region_15.16_spmd, body=%wide.region_13.15_spmd.sunk | while | flops 2064971776 | bytes 151884048 | solution.py:164
  569.0 1.8 fusion.114
  570.8 4.3 fusion.115
  575.1 4.8 multiply_reduce_fusion.5
  579.9 5.6 multiply_convert_fusion.4
  585.5 4.1 fusion.117
  590.1 2.0 fusion.116
  594.6 1.8 fusion.114
  596.5 4.3 fusion.115
  600.8 4.8 multiply_reduce_fusion.5
  605.5 5.6 multiply_convert_fusion.4
  611.2 4.1 fusion.117
  615.8 2.0 fusion.116
  619.4 4.1 copy.47
  624.7 4.0 convolution_convert_fusion.2
  629.0 7.1 fusion.71
  636.1 4.2 fusion.72
  641.9 5.3 fusion.40
  649.5 14.6 %all-reduce.1 = (f32[2,192]{1,0:T(2,128)}, f32[768]{0:T(1024)}) all-reduce(f32[2,192]{1,0:T(2,128)S(1)} %pad_maximum_fusion.1, f32[768]{0:T(1024)S(1)} %copy-done.60), channel_id=1, replica_groups=mesh['dp'=8,'tp'=4] {'dp'}, use_global_device_ids=true, to_apply=%region_27.28 | all-reduce | flops 1152 | bytes 9216 | tf_op jit(solution)/shard_map/psum | solution.py:184
  664.2 23.7 %reduce-scatter.11.cloned.1.call-done = bf16[512,768]{1,0:T(8,128)(2,1)} async-done(((bf16[2048,768]{1,0:T(8,128)(2,1)}), bf16[512,768]{1,0:T(8,128)(2,1)}) %reduce-scatter.11.cloned.1.call-update) | async-done | bytes 786448 | tf_op jit(solution)/shard_map/reduce_scatter | solution.py:177
  688.0 2.1 fusion.50
  690.0 2.1 fusion.65
  693.8 41.7 %all-reduce = (f32[768]{0:T(1024)}, f32[768]{0:T(1024)}, f32[768]{0:T(1024)}, f32[768]{0:T(1024)}, f32[768]{0:T(1024)}, /*index=5*/f32[768]{0:T(1024)}, f32[768]{0:T(1024)}) all-reduce(f32[768]{0:T(1024)S(1)} %get-tuple-element.105, f32[768]{0:T(1024)S(1)} %get-tuple-element.102, ...), channel_id=1, replica_groups=mesh['dp'=8,'tp'=4] {'dp','tp'}, use_global_device_ids=true, to_apply=%region_20.21 | all-reduce | flops 5376 | bytes 43008 | tf_op jit(solution)/shard_map/psum | solution.py:195
  735.4 70.6 %all-reduce.5.cloned.1.call-done = (f32[768,3,192]{0,2,1:T(8,128)}, f32[192,768]{1,0:T(8,128)}, f32[768,768]{1,0:T(8,128)}, f32[768,768]{1,0:T(8,128)}) async-done(((f32[768,3,192]{0,2,1:T(8,128)}, f32[192,768]{1,0:T(8,128)}, f32[768,768]{1,0:T(8,128)}, f32[768,768]{1,0:T(8,128)}), (f32[768,3,192]{0,2,1:T(8,128)}, f32[192,768]{1,0:T(8,128)}, f32[768,768]{1,0:T(8,128)}, ...) | async-done | bytes 7077904 | tf_op jit(solution)/shard_map/psum | solution.py:184
  806.0 2.9 copy.82
  (211 shorter events, 33.3 us)
Async XLA Ops:
  7.2 337.5 %copy-start = (bf16[768,768]{1,0:T(8,128)(2,1)S(1)}, bf16[768,768]{1,0:T(8,128)(2,1)}, u32[]{:S(2)}) copy-start(bf16[768,768]{1,0:T(8,128)(2,1)} %param.35) | copy-start | bytes 3538948
  7.2 201.6 %reduce-scatter.5.cloned.1.call-start = ((), (), s32[]{:S(2)}) async-start(), calls=%async_computation.4 | async-start | bytes 3932160 | tf_op jit(solution)/shard_map/reduce_scatter | solution.py:134
  8.1 484.3 %copy-start.30 = (f32[512]{0:T(512)}, f32[512]{0:T(512)S(1)}, u32[]{:S(2)}) copy-start(f32[512]{0:T(512)S(1)} %get-tuple-element.151) | copy-start | bytes 6148
  8.8 483.7 %copy-start.32 = (f32[512]{0:T(512)}, f32[512]{0:T(512)S(1)}, u32[]{:S(2)}) copy-start(f32[512]{0:T(512)S(1)} %convert_multiply_fusion.5) | copy-start | bytes 6148
  10.4 7.4 copy-start.43
  12.1 5.7 copy-start.52
  12.1 5.7 copy-start.46
  12.1 28.1 %copy-start.61 = (f32[2,192]{1,0:T(2,128)S(1)}, f32[2,192]{1,0:T(2,128)}, u32[]{:S(2)}) copy-start(f32[2,192]{1,0:T(2,128)} %param.28) | copy-start | bytes 4612
  14.7 20.8 %collective-permute-start = (bf16[512,768]{1,0:T(8,128)(2,1)S(1)}, bf16[512,768]{1,0:T(8,128)(2,1)}, u32[]{:S(2)}, u32[]{:S(2)}) collective-permute-start(bf16[512,768]{1,0:T(8,128)(2,1)S(1)} %add_convert_fusion.3), channel_id=1, source_target_pairs={{0,1},{1,0},{2,3},{3,2},{4,5},{5,4},{6,7},{7,6},{8,9},{9,8},{10,11... | collective-permute-start | bytes 2359304 | tf_op jit(solution)/shard_map/ppermute | solution.py:13
  37.4 3.0 copy-start.23
  37.4 70.3 %collective-permute-start.1 = (bf16[1024,768]{1,0:T(8,128)(2,1)S(1)}, bf16[1024,768]{1,0:T(8,128)(2,1)}, u32[]{:S(2)}, u32[]{:S(2)}) collective-permute-start(bf16[1024,768]{1,0:T(8,128)(2,1)S(1)} %maximum_select_fusion.1), channel_id=1, source_target_pairs={{0,2},{1,3},{2,0},{3,1},{4,6},{5,7},{6,4},{7,5},{8,10},{9,11},{10,... | collective-permute-start | bytes 4718600 | tf_op jit(solution)/shard_map/ppermute | solution.py:13
  121.8 3.2 copy-start.25
  125.0 3.2 copy-start.37
  132.9 3.2 copy-start.25
  136.1 3.2 copy-start.37
  140.8 2.8 copy-start.5
  140.8 3.7 copy-start.35
  147.2 61.6 %copy-start.3 = (bf16[512,768]{1,0:T(8,128)(2,1)S(1)}, bf16[512,768]{1,0:T(8,128)(2,1)}, u32[]{:S(2)}) copy-start(bf16[512,768]{1,0:T(8,128)(2,1)} %param.21) | copy-start | bytes 2359300
  147.2 61.6 %copy-start.28 = (f32[768]{0:T(1024)S(1)}, f32[768]{0:T(1024)}, u32[]{:S(2)}) copy-start(f32[768]{0:T(1024)} %param.24) | copy-start | bytes 9220
  147.2 61.6 %copy-start.39 = (f32[768]{0:T(1024)S(1)}, f32[768]{0:T(1024)}, u32[]{:S(2)}) copy-start(f32[768]{0:T(1024)} %param.30) | copy-start | bytes 9220
  147.2 133.2 %all-gather.4.cloned.1.call-start = ((), (), s32[]{:S(2)}) async-start(), calls=%async_computation.5 | async-start | bytes 3932160 | tf_op jit(solution)/shard_map/all_gather | solution.py:140
  208.8 5.1 copy-start.7
  210.7 2.6 copy-start.40
  210.7 6.3 copy-start.20
  216.9 127.8 %all-gather.6.cloned.1.call-start = ((), (), s32[]{:S(2)}) async-start(), calls=%async_computation.7 | async-start | bytes 3932160 | tf_op jit(solution)/shard_map/all_gather | solution.py:149
  218.8 211.2 %reduce-scatter.9.cloned.1.call-start = ((), (), s32[]{:S(2)}) async-start(), calls=%async_computation.8 | async-start | bytes 3932160 | tf_op jit(solution)/shard_map/reduce_scatter | solution.py:155
  344.7 22.0 %copy-start.63 = (bf16[768,768]{1,0:T(8,128)(2,1)S(1)}, bf16[768,768]{1,0:T(8,128)(2,1)}, u32[]{:S(2)}) copy-start(bf16[768,768]{1,0:T(8,128)(2,1)} %param.33) | copy-start | bytes 3538948
  370.7 121.7 %reduce-scatter.7.cloned.1.call-start = ((), (), s32[]{:S(2)}) async-start(), calls=%async_computation.6 | async-start | bytes 3932160 | tf_op jit(solution)/shard_map/reduce_scatter | solution.py:145
  382.7 47.3 %copy-start.41 = (f32[512]{0:T(512)S(1)}, f32[512]{0:T(512)}, u32[]{:S(2)}) copy-start(f32[512]{0:T(512)} %copy-done.40) | copy-start | bytes 6148
  382.7 47.3 %copy-start.42 = (f32[768]{0:T(1024)S(1)}, f32[768]{0:T(1024)}, u32[]{:S(2)}) copy-start(f32[768]{0:T(1024)} %param.31) | copy-start | bytes 9220
  382.7 50.1 %copy-start.55 = (f32[512]{0:T(512)S(1)}, f32[512]{0:T(512)}, u32[]{:S(2)}) copy-start(f32[512]{0:T(512)} %copy-done.54) | copy-start | bytes 6148
  382.7 50.1 %copy-start.49 = (f32[512]{0:T(512)S(1)}, f32[512]{0:T(512)}, u32[]{:S(2)}) copy-start(f32[512]{0:T(512)} %copy-done.48) | copy-start | bytes 6148
  382.7 109.8 %copy-start.51 = (f32[512]{0:T(512)S(1)}, f32[512]{0:T(512)}, u32[]{:S(2)}) copy-start(f32[512]{0:T(512)} %copy-done.50) | copy-start | bytes 6148
  382.7 109.8 %copy-start.59 = (f32[768]{0:T(1024)S(1)}, f32[768]{0:T(1024)}, u32[]{:S(2)}) copy-start(f32[768]{0:T(1024)} %param.36) | copy-start | bytes 9220
  382.7 177.4 %all-gather.8.cloned.1.call-start = ((), (), s32[]{:S(2)}) async-start(), calls=%async_computation.9 | async-start | bytes 3932160 | tf_op jit(solution)/shard_map/all_gather | solution.py:161
  430.0 2.9 copy-start.15
  434.6 125.5 %copy-start.36 = (bf16[192,768]{1,0:T(8,128)(2,1)S(1)}, bf16[192,768]{1,0:T(8,128)(2,1)}, u32[]{:S(2)}) copy-start(bf16[192,768]{1,0:T(8,128)(2,1)} %param.29) | copy-start | bytes 884740
  496.7 191.3 %reduce-scatter.11.cloned.1.call-start = ((), (), s32[]{:S(2)}) async-start(), calls=%async_computation.10 | async-start | bytes 3932160 | tf_op jit(solution)/shard_map/reduce_scatter | solution.py:177
  564.1 3.8 copy-start.6
  564.1 3.8 copy-start.34
  585.5 4.6 copy-start.2
  590.1 2.0 copy-start.10
  590.1 2.1 copy-start.12
  611.2 4.6 copy-start.2
  615.8 2.1 copy-start.10
  615.8 2.1 copy-start.12
  628.7 177.3 %all-reduce.5.cloned.1.call-start = ((), (), s32[]{:S(2)}) async-start(), calls=%async_computation.11 | async-start | bytes 14155776 | tf_op jit(solution)/shard_map/psum | solution.py:184
  629.0 7.1 copy-start.19
  629.0 7.1 copy-start.62
  636.1 4.2 copy-start.9
  636.1 4.2 copy-start.17
  648.8 39.1 %copy-start.4 = (bf16[512,768]{1,0:T(8,128)(2,1)S(1)}, bf16[512,768]{1,0:T(8,128)(2,1)}, u32[]{:S(2)}) copy-start(bf16[512,768]{1,0:T(8,128)(2,1)} %param.21) | copy-start | bytes 2359300
  648.8 39.1 %copy-start.29 = (f32[768]{0:T(1024)S(1)}, f32[768]{0:T(1024)}, u32[]{:S(2)}) copy-start(f32[768]{0:T(1024)} %param.24) | copy-start | bytes 9220
  648.9 39.1 %copy-start.31 = (f32[512]{0:T(512)S(1)}, f32[512]{0:T(512)}, u32[]{:S(2)}) copy-start(f32[512]{0:T(512)} %copy-done.30) | copy-start | bytes 6148
  648.9 39.1 %copy-start.33 = (f32[512]{0:T(512)S(1)}, f32[512]{0:T(512)}, u32[]{:S(2)}) copy-start(f32[512]{0:T(512)} %copy-done.32) | copy-start | bytes 6148
  648.9 39.1 %copy-start.44 = (f32[512]{0:T(512)S(1)}, f32[512]{0:T(512)}, u32[]{:S(2)}) copy-start(f32[512]{0:T(512)} %copy-done.43) | copy-start | bytes 6148
  648.9 39.1 %copy-start.45 = (f32[768]{0:T(1024)S(1)}, f32[768]{0:T(1024)}, u32[]{:S(2)}) copy-start(f32[768]{0:T(1024)} %param.25) | copy-start | bytes 9220
  648.9 39.1 %copy-start.47 = (f32[512]{0:T(512)S(1)}, f32[512]{0:T(512)}, u32[]{:S(2)}) copy-start(f32[512]{0:T(512)} %copy-done.46) | copy-start | bytes 6148
  648.9 41.1 %copy-start.53 = (f32[512]{0:T(512)S(1)}, f32[512]{0:T(512)}, u32[]{:S(2)}) copy-start(f32[512]{0:T(512)} %copy-done.52) | copy-start | bytes 6148
  664.2 28.0 %copy-start.16 = (f32[512,768]{1,0:T(8,128)S(1)}, f32[512,768]{1,0:T(8,128)}, u32[]{:S(2)}) copy-start(f32[512,768]{1,0:T(8,128)} %get-tuple-element.150) | copy-start | bytes 4718596
  806.0 3.0 copy-start.27
  806.0 3.8 copy-start.22
  809.8 2.5 copy-start.21
  809.8 3.9 copy-start.1
  (21 other events, 25.6 us)
Sparse Core Ops, SparseCore 0:
  147.3 61.3 reduce-scatter.4
  217.1 63.3 all-gather.3
  282.6 62.0 all-gather.5
  370.9 59.0 reduce-scatter.8
  432.1 60.3 reduce-scatter.6
  496.8 63.3 all-gather.7
  628.8 59.0 reduce-scatter.10
  692.7 113.2 all-reduce.4
